TPU v7x, 32 devices: a whole 2x2x4 slice. The times are simulated.
32 devices in a mesh: seq: 8 (over y, x, core), tensor: 4 (over z).
Axes of the slice: x: 2, y: 2, z: 4, core: 2. Of those that a mesh axis runs over, the one named last changes fastest.
Arguments:
- streams: float32 [4, 4096, 4096], P(None, 'seq', 'tensor'), may hold values from -8 to 8
- mix_weight: float32 [24, 4, 4096], P(None, None, 'tensor'), may hold values from -0.046875 to 0.046875
- mix_bias: float32 [24], replicated, may hold values from -4 to 4
- mix_scale: float32 [3], replicated, may hold values from 1 to 2
- norm_gain: bfloat16 [4096], replicated, may hold values from 0.25 to 1.75
- gate_weight: bfloat16 [4096, 7168], P('seq', 'tensor'), may hold values from -0.09375 to 0.09375
- up_weight: bfloat16 [4096, 7168], P('seq', 'tensor'), may hold values from -0.09375 to 0.09375
- down_weight: bfloat16 [7168, 4096], P('tensor', 'seq'), may hold values from -0.0625 to 0.0625
Outputs:
- new_streams: float32 [4, 4096, 4096], P(None, 'seq', 'tensor')
All inputs are finite; a program needn't handle non-finite values.
Results may differ from a plain program's by a relative error of at most 0.01.
Values may be sent and summed in bfloat16 or wider, within the bound.
A program may use at most 128 MiB of HBM per device.

v0:
```python
import jax
import jax.numpy as jnp
from jax import lax
from jax.sharding import PartitionSpec as P

D = 4096
STREAMS = 4
SWEEPS = 20
epsilon = 0.25


def coefficients(logits, mix_bias, mix_scale):
    pre_mix = jax.nn.sigmoid(mix_scale[0] * logits[:STREAMS] + mix_bias[:STREAMS, None])
    post_mix = 2.0 * jax.nn.sigmoid(
        mix_scale[1] * logits[STREAMS : 2 * STREAMS] + mix_bias[STREAMS : 2 * STREAMS, None]
    )
    start_mix = jnp.exp(mix_scale[2] * logits[2 * STREAMS :] + mix_bias[2 * STREAMS :, None])
    start_mix = start_mix.reshape(STREAMS, STREAMS, logits.shape[1])

    def balance(iteration, matrix):
        matrix = matrix / jnp.sum(matrix, axis=1, keepdims=True)
        return matrix / jnp.sum(matrix, axis=0, keepdims=True)

    return (pre_mix, post_mix, lax.fori_loop(0, SWEEPS, balance, start_mix))


def project_logits(mix_weight, values):
    return jnp.einsum("lkd,ktd->lt", mix_weight, values, precision=lax.Precision.HIGHEST)


def add_rows(normed, segment):
    return jnp.dot(normed, segment, preferred_element_type=jnp.float32)


def body(streams, mix_weight, mix_bias, mix_scale, norm_gain, gate_weight, up_weight, down_weight):
    feature_count = STREAMS * D
    squares = jnp.sum(streams * streams, axis=(0, 2))[None, :]
    raw_logits = project_logits(mix_weight, streams)
    totals, raw_sums = (
        lax.psum(squares.astype(jnp.bfloat16), "tensor").astype(jnp.float32),
        lax.psum(raw_logits.astype(jnp.bfloat16), "tensor").astype(jnp.float32),
    )
    logits = raw_sums * lax.rsqrt(totals / feature_count + epsilon)
    pre_mix, post_mix, res_mix = coefficients(logits, mix_bias, mix_scale)
    layer_in = jnp.sum(pre_mix[:, :, None] * streams, axis=0).astype(jnp.bfloat16)
    whole_input = lax.all_gather(layer_in, "tensor", axis=1, tiled=True)
    as_float = whole_input.astype(jnp.float32)
    mean_square = jnp.mean(as_float * as_float, axis=1, keepdims=True)
    normed = (as_float * lax.rsqrt(mean_square + epsilon) * norm_gain.astype(jnp.float32)).astype(
        jnp.bfloat16
    )

    def add_single(segment):
        return add_rows(normed, segment)

    gate_value = add_single(lax.all_gather(gate_weight, "seq", axis=0, tiled=True))
    up_value = add_single(lax.all_gather(up_weight, "seq", axis=0, tiled=True))
    hidden = (jax.nn.silu(gate_value) * up_value).astype(jnp.bfloat16)
    partial_out = jnp.dot(
        hidden,
        lax.all_gather(down_weight, "seq", axis=1, tiled=True),
        preferred_element_type=jnp.float32,
    )
    layer_out = lax.psum_scatter(
        partial_out.astype(jnp.bfloat16), "tensor", scatter_dimension=1, tiled=True
    ).astype(jnp.float32)
    outputs = []
    for target in range(STREAMS):
        mixed = post_mix[target][:, None] * layer_out
        for source in range(STREAMS):
            mixed = mixed + res_mix[target, source][:, None] * streams[source]
        outputs.append(mixed)
    return jnp.stack(outputs)


def solution(mesh):
    placed = (
        P(None, "seq", "tensor"),
        P(None, None, "tensor"),
        P(),
        P(),
        P(),
        P("seq", "tensor"),
        P("seq", "tensor"),
        P("tensor", "seq"),
    )
    return jax.shard_map(
        body, mesh=mesh, in_specs=placed, out_specs=P(None, "seq", "tensor"), check_vma=False
    )
```

profile of v0, /device:TPU:0, one launch (start us, length us, event | category | flops | bytes accessed | tf_op | source)
XLA Modules:
  0.0 502.4 jit_solution(2445068829800795499)
XLA Ops:
  6.5 0.0 all-gather.5.cloned.1.call-start
  6.5 0.0 copy-start
  6.5 4.2 multiply_reduce_fusion.1
  10.7 1.6 copy-done
  12.3 0.0 copy-start.3
  12.3 0.0 copy-start.4
  12.3 8.1 %fusion.28 = bf16[24,512]{1,0:T(8,128)(2,1)S(1)} fusion(f32[4,512,1024]{2,1,0:T(8,128)S(1)} %copy-done, f32[24,4,1024]{2,1,0:T(4,128)} %param.11), kind=kOutput, calls=%fused_computation.55 | convolution fusion | flops 603992064 | bytes 8806400 | tf_op jit(solution)/shard_map/lkd,ktd->lt/dot_general | solution.py:28
  20.5 20.8 %all-reduce = (bf16[24,512]{1,0:T(8,128)(2,1)S(1)}, bf16[1,512]{1,0:T(2,128)(2,1)S(1)}) all-reduce(bf16[24,512]{1,0:T(8,128)(2,1)S(1)} %fusion.28, bf16[1,512]{1,0:T(2,128)(2,1)S(1)} %convert_element_type.47), channel_id=1, replica_groups=mesh['seq'=8,'tensor'=4] {'tensor'}, use_global_device_ids=true, to_apply=%region_0.0 | all-reduce | flops 12800 | bytes 51200 | tf_op jit(solution)/shard_map/psum | solution.py:41
  41.3 0.0 copy-done.3
  41.3 0.7 fusion.46
  42.0 0.0 copy-done.4
  42.0 0.1 fusion.47
  42.0 1.4 fusion.42
  43.5 5.3 %multiply_reduce_fusion = bf16[512,1024]{1,0:T(8,128)(2,1)} fusion(f32[4,512,1024]{2,1,0:T(8,128)} %param.10, f32[4,512]{1,0:T(4,128)S(1)} %get-tuple-element.29), kind=kLoop, calls=%fused_computation.8 | loop fusion | flops 3670016 | bytes 9445376 | tf_op jit(solution)/shard_map/reduce_sum | solution.py:45
  48.7 0.0 all-gather.5.cloned.1.call-update
  48.7 0.0 all-gather.7.cloned.1.call-start
  48.8 0.7 all-gather.7.cloned.1.call-update
  49.5 0.0 copy-start.2
  49.5 0.0 all-gather.11.cloned.1.call-start
  49.5 0.7 all-gather.11.cloned.1.call-update
  50.2 0.0 all-gather.9.cloned.1.call-start
  50.3 0.5 all-gather.9.cloned.1.call-update
  50.8 0.0 reduce-scatter.2.cloned.1.call-start
  50.9 0.0 copy-done.2
  50.9 77.0 %all-gather.5.cloned.1.call-done = bf16[512,4096]{1,0:T(8,128)(2,1)} async-done(((bf16[512,1024]{1,0:T(8,128)(2,1)}), bf16[512,4096]{1,0:T(8,128)(2,1)}) %all-gather.5.cloned.1.call-update) | async-done | bytes 4194320 | tf_op jit(solution)/shard_map/all_gather | solution.py:46
  127.9 3.1 fusion
  131.0 78.2 %all-gather.7.cloned.1.call-done = bf16[4096,1792]{1,0:T(8,128)(2,1)} async-done(((bf16[512,1792]{1,0:T(8,128)(2,1)}), bf16[4096,1792]{1,0:T(8,128)(2,1)}) %all-gather.7.cloned.1.call-update) | async-done | bytes 14680080 | tf_op jit(solution)/shard_map/all_gather | solution.py:56
  209.1 14.7 %fusion.26 = f32[512,1792]{1,0:T(8,128)} fusion(bf16[4096,1792]{1,0:T(8,128)(2,1)} %all-gather.7.cloned.1.call-done, bf16[512,4096]{1,0:T(8,128)(2,1)} %all-gather.5.cloned.1.call-done, f32[4096]{0:T(1024)S(1)} %convert_element_type.51, f32[512]{0:T(512)S(1)} %add_rsqrt_fusion), kind=kOutput, calls=%fused_computation.53 | convolution fusion | flops 7524581376 | bytes 22562816 | tf_op jit(solution)/shard_map/dot_general | solution.py:32
  223.8 70.9 %all-gather.11.cloned.1.call-done = bf16[1792,4096]{1,0:T(8,128)(2,1)} async-done(((bf16[1792,512]{1,0:T(8,128)(2,1)}), bf16[1792,4096]{1,0:T(8,128)(2,1)}) %all-gather.11.cloned.1.call-update) | async-done | bytes 14680080 | tf_op jit(solution)/shard_map/all_gather | solution.py:61
  294.8 82.6 %all-gather.9.cloned.1.call-done = bf16[4096,1792]{1,0:T(8,128)(2,1)} async-done(((bf16[512,1792]{1,0:T(8,128)(2,1)}), bf16[4096,1792]{1,0:T(8,128)(2,1)}) %all-gather.9.cloned.1.call-update) | async-done | bytes 14680080 | tf_op jit(solution)/shard_map/all_gather | solution.py:57
  377.4 28.8 %convolution_convert_fusion = bf16[512,4096]{1,0:T(8,128)(2,1)} fusion(bf16[1792,4096]{1,0:T(8,128)(2,1)} %all-gather.11.cloned.1.call-done, f32[512,1792]{1,0:T(8,128)} %fusion.26, bf16[4096,1792]{1,0:T(8,128)(2,1)} %all-gather.9.cloned.1.call-done, bf16[512,4096]{1,0:T(8,128)(2,1)} %all-gather.5.cloned.1.call-done, f32[4096]{0:T(1024)S(1)} %convert_element_type.51, ...), kind=kOutput, calls=%fused_computation.10 | convolution fusion | flops 15048376320 | bytes 41437184 | tf_op jit(solution)/shard_map/dot_general | solution.py:59
  406.2 0.0 reduce-scatter.2.cloned.1.call-update
  406.2 0.1 slice.120
  406.3 0.8 fusion.31
  407.1 2.1 while.10
  409.3 73.9 %reduce-scatter.2.cloned.1.call-done = bf16[512,1024]{1,0:T(8,128)(2,1)} async-done(((bf16[512,4096]{1,0:T(8,128)(2,1)}), bf16[512,1024]{1,0:T(8,128)(2,1)}) %reduce-scatter.2.cloned.1.call-update) | async-done | bytes 1048592 | tf_op jit(solution)/shard_map/reduce_scatter | solution.py:64
  483.2 0.0 copy-start.1
  483.2 4.7 fusion.7
  487.8 0.0 copy-done.1
  487.8 4.3 fusion.17
  492.1 3.7 pad_maximum_fusion
  (68 shorter events, 1.8 us)
Async XLA Ops:
  6.5 121.3 %all-gather.5.cloned.1.call-start = ((), (), s32[]{:S(2)}) async-start(), calls=%async_computation.1 | async-start | bytes 5242880 | tf_op jit(solution)/shard_map/all_gather | solution.py:46
  6.5 5.8 %copy-start = (f32[4,512,1024]{2,1,0:T(8,128)S(1)}, f32[4,512,1024]{2,1,0:T(8,128)}, u32[]{:S(2)}) copy-start(f32[4,512,1024]{2,1,0:T(8,128)} %param.10) | copy-start | bytes 25165828
  12.3 29.0 %copy-start.3 = (f32[3]{0:T(128)S(1)}, f32[3]{0:T(128)}, u32[]{:S(2)}) copy-start(f32[3]{0:T(128)} %param.13) | copy-start | bytes 40
  12.3 29.7 %copy-start.4 = (f32[24]{0:T(128)S(1)}, f32[24]{0:T(128)}, u32[]{:S(2)}) copy-start(f32[24]{0:T(128)} %param.12) | copy-start | bytes 292
  48.7 160.4 %all-gather.7.cloned.1.call-start = ((), (), s32[]{:S(2)}) async-start(), calls=%async_computation.2 | async-start | bytes 16515072 | tf_op jit(solution)/shard_map/all_gather | solution.py:56
  49.5 1.4 copy-start.2
  49.5 245.3 %all-gather.11.cloned.1.call-start = ((), (), s32[]{:S(2)}) async-start(), calls=%async_computation.4 | async-start | bytes 16515072 | tf_op jit(solution)/shard_map/all_gather | solution.py:61
  50.2 327.2 %all-gather.9.cloned.1.call-start = ((), (), s32[]{:S(2)}) async-start(), calls=%async_computation.3 | async-start | bytes 16515072 | tf_op jit(solution)/shard_map/all_gather | solution.py:57
  50.8 432.3 %reduce-scatter.2.cloned.1.call-start = ((), (), s32[]{:S(2)}) async-start(), calls=%async_computation.5 | async-start | bytes 5242880 | tf_op jit(solution)/shard_map/reduce_scatter | solution.py:64
  483.2 4.7 copy-start.1
Sparse Core Ops, SparseCore 0:
  48.9 78.9 all-gather.4
  129.8 79.3 all-gather.6
  211.0 83.7 all-gather.10
  296.5 80.8 all-gather.8
  406.3 76.7 reduce-scatter.1
where the time goes:
time: 503 us; the launch traced here: 502 us
  waiting for transfers between devices  385 us (77%)
  matrix products  51.6 us (10%)
  other arithmetic  29.1 us (6%)
  blocking collectives  20.8 us (4%)
  between operations  13.3 us (3%)
    all_gather x1, waiting for transfers between devices, body(): up_value = add_single(lax.all_gather(up_weight, 'seq', axis=0, tiled=True))  82.6 us
    all_gather x1, waiting for transfers between devices, body(): lax.all_gather(gate_weight, 'seq', axis=0, tiled=True)  78.2 us
    all_gather x1, waiting for transfers between devices, body(): whole_input = lax.all_gather(layer_in, 'tensor', axis=1, tiled=True)  77 us
    reduce_scatter x1, waiting for transfers between devices, body(): lax.psum_scatter(partial_out.astype(jnp.bfloat16), 'tensor', scatter_dime...  73.9 us
    all_gather x1, waiting for transfers between devices, body(): lax.all_gather(down_weight, 'seq', axis=1, tiled=True)  70.9 us
    dot_general x1, matrix products, body(): jnp.dot(hidden, lax.all_gather(down_weight, 'seq', axis=1, tiled=True), p...  28.8 us
    psum x1, blocking collectives, body(): lax.psum(raw_logits.astype(jnp.bfloat16), 'tensor').astype(jnp.float32)  20.8 us
    dot_general x1, matrix products, add_rows(): return jnp.dot(normed, segment, preferred_element_type=jnp.float32)  14.7 us
  transfers between devices with their start and end apart: 5, of which 5 were waited for; matrix products, arithmetic and copies ran while one was open for 4% of the time, Pallas kernels for 0%

commit v1 on v0

--- a/solution.py
+++ b/solution.py
@@ -7,6 +7,16 @@
 STREAMS = 4
 SWEEPS = 20
 epsilon = 0.25
+
+
+def gather_by_hops(shard, axis, along):
+    size = lax.axis_size(axis)
+    held, blocks = (shard, [shard])
+    for _ in range(size - 1):
+        held = lax.ppermute(held, axis, [(i, (i + 1) % size) for i in range(size)])
+        blocks.insert(0, held)
+    line = jnp.concatenate(blocks, axis=along)
+    return jnp.roll(line, (lax.axis_index(axis) + 1) * shard.shape[along], axis=along)
 
 
 def coefficients(logits, mix_bias, mix_scale):
@@ -43,7 +53,7 @@
     logits = raw_sums * lax.rsqrt(totals / feature_count + epsilon)
     pre_mix, post_mix, res_mix = coefficients(logits, mix_bias, mix_scale)
     layer_in = jnp.sum(pre_mix[:, :, None] * streams, axis=0).astype(jnp.bfloat16)
-    whole_input = lax.all_gather(layer_in, "tensor", axis=1, tiled=True)
+    whole_input = gather_by_hops(layer_in, "tensor", 1)
     as_float = whole_input.astype(jnp.float32)
     mean_square = jnp.mean(as_float * as_float, axis=1, keepdims=True)
     normed = (as_float * lax.rsqrt(mean_square + epsilon) * norm_gain.astype(jnp.float32)).astype(

time: 503 us -> 386 us (0.77)
  waiting for transfers between devices: 385 us -> 265 us
  local copies, waits for them, and re-layouts: 2.49 us -> 11.4 us
  other arithmetic: 29.1 us -> 23.7 us
    all_gather x1, waiting for transfers between devices: 78.2 us -> 0.02 us  [body(): lax.all_gather(gate_weight, 'seq', axis=0, tiled=True)]
    all_gather x1 -> x0, waiting for transfers between devices: 77 us -> none  [body(): whole_input = lax.all_gather(layer_in, 'tensor', axis=1, tiled=True)]
    ppermute x0 -> x3, waiting for transfers between devices: none -> 67.9 us  [gather_by_hops(): held = lax.ppermute(held, axis, [(i, (i + 1) % size) for i in range(size)])]
    all_gather x1, waiting for transfers between devices: 82.6 us -> 35.8 us  [body(): up_value = add_single(lax.all_gather(up_weight, 'seq', axis=0, tiled=True))]
    all_gather x1, waiting for transfers between devices: 70.9 us -> 85.6 us  [body(): lax.all_gather(down_weight, 'seq', axis=1, tiled=True)]
    unnamed x10 -> x31, local copies, waits for them, and re-layouts: 1.62 us -> 10.4 us
  transfers between devices with their start and end apart: 5 -> 7, of which waited for: 5 -> 6; matrix products, arithmetic and copies ran while one was open for 4% -> 10% of each run, Pallas kernels for 0% -> 0%
where the time goes in v1:
time: 386 us; the launch traced here: 385 us
  waiting for transfers between devices  265 us (69%)
  matrix products  50.8 us (13%)
  other arithmetic  23.7 us (6%)
  blocking collectives  20.8 us (5%)
  between operations  13.4 us (3%)
  local copies, waits for them, and re-layouts  11.4 us (3%)
    all_gather x1, waiting for transfers between devices, body(): lax.all_gather(down_weight, 'seq', axis=1, tiled=True)  85.6 us
    reduce_scatter x1, waiting for transfers between devices, body(): lax.psum_scatter(partial_out.astype(jnp.bfloat16), 'tensor', scatter_dime...  73.2 us
    ppermute x3, waiting for transfers between devices, gather_by_hops(): held = lax.ppermute(held, axis, [(i, (i + 1) % size) for i in range(size)])  67.9 us
    all_gather x1, waiting for transfers between devices, body(): up_value = add_single(lax.all_gather(up_weight, 'seq', axis=0, tiled=True))  35.8 us
    dot_general x1, matrix products, body(): jnp.dot(hidden, lax.all_gather(down_weight, 'seq', axis=1, tiled=True), p...  28.8 us
    psum x1, blocking collectives, body(): lax.psum(raw_logits.astype(jnp.bfloat16), 'tensor').astype(jnp.float32)  20.8 us
    dot_general x1, matrix products, add_rows(): return jnp.dot(normed, segment, preferred_element_type=jnp.float32)  14.9 us
    unnamed x31, local copies, waits for them, and re-layouts  10.4 us
  transfers between devices with their start and end apart: 7, of which 6 were waited for; matrix products, arithmetic and copies ran while one was open for 10% of the time, Pallas kernels for 0%

profile of v1, /device:TPU:0, one launch (start us, length us, event | category | flops | bytes accessed | tf_op | source)
XLA Modules:
  0.0 385.4 jit_solution(5117807169956732216)
XLA Ops:
  6.5 0.0 all-gather.4.cloned.1.call-start
  6.5 0.7 all-gather.4.cloned.1.call-update
  7.3 0.0 all-gather.6.cloned.1.call-start
  7.3 0.7 all-gather.6.cloned.1.call-update
  8.0 0.0 all-gather.8.cloned.1.call-start
  8.1 0.0 copy-start.4
  8.1 0.7 all-gather.8.cloned.1.call-update
  8.7 0.0 reduce-scatter.2.cloned.1.call-start
  8.8 0.0 copy-start
  8.8 4.2 %multiply_reduce_fusion.1 = bf16[512]{0:T(512)(128)(2,1)S(1)} fusion(f32[4,512,1024]{2,1,0:T(8,128)} %param.10), kind=kLoop, calls=%fused_computation.9 | loop fusion | flops 4193792 | bytes 8389632 | tf_op jit(solution)/shard_map/reduce_sum | solution.py:47
  13.0 0.0 copy-done.4
  13.0 1.6 copy-done
  14.6 0.0 copy-start.9
  14.6 0.0 copy-start.10
  14.6 7.2 %fusion.24 = bf16[24,512]{1,0:T(8,128)(2,1)S(1)} fusion(f32[4,512,1024]{2,1,0:T(8,128)S(1)} %copy-done, f32[24,4,1024]{2,1,0:T(4,128)S(1)} %copy-done.4), kind=kOutput, calls=%fused_computation.54 | convolution fusion | flops 603992064 | bytes 8806400 | tf_op jit(solution)/shard_map/lkd,ktd->lt/dot_general | solution.py:38
  21.8 20.8 %all-reduce = (bf16[24,512]{1,0:T(8,128)(2,1)S(1)}, bf16[1,512]{1,0:T(2,128)(2,1)S(1)}) all-reduce(bf16[24,512]{1,0:T(8,128)(2,1)S(1)} %fusion.24, bf16[1,512]{1,0:T(2,128)(2,1)S(1)} %convert_element_type.47), channel_id=1, replica_groups=mesh['seq'=8,'tensor'=4] {'tensor'}, use_global_device_ids=true, to_apply=%region_0.0 | all-reduce | flops 12800 | bytes 51200 | tf_op jit(solution)/shard_map/psum | solution.py:51
  42.6 0.0 copy-done.9
  42.6 0.7 fusion.49
  43.2 0.0 copy-done.10
  43.2 0.1 fusion.50
  43.3 0.0 copy-start.5
  43.3 2.0 fusion.42
  45.3 0.0 copy-done.5
  45.3 4.1 %multiply_reduce_fusion = bf16[512,1024]{1,0:T(8,128)(2,1)S(1)} fusion(f32[4,512,1024]{2,1,0:T(8,128)} %param.10, f32[4,512]{1,0:T(4,128)S(1)} %get-tuple-element.29), kind=kLoop, calls=%fused_computation.8 | loop fusion | flops 3670016 | bytes 9445376 | tf_op jit(solution)/shard_map/reduce_sum | solution.py:55
  49.4 0.1 collective-permute-start
  49.5 23.3 %collective-permute-done = bf16[512,1024]{1,0:T(8,128)(2,1)S(1)} collective-permute-done((bf16[512,1024]{1,0:T(8,128)(2,1)S(1)}, bf16[512,1024]{1,0:T(8,128)(2,1)S(1)}, u32[]{:S(2)}, u32[]{:S(2)}) %collective-permute-start) | collective-permute-done | bytes 1048608 | tf_op jit(solution)/shard_map/ppermute | solution.py:16
  72.8 0.0 collective-permute-start.1
  72.8 23.3 %collective-permute-done.1 = bf16[512,1024]{1,0:T(8,128)(2,1)S(1)} collective-permute-done((bf16[512,1024]{1,0:T(8,128)(2,1)S(1)}, bf16[512,1024]{1,0:T(8,128)(2,1)S(1)}, u32[]{:S(2)}, u32[]{:S(2)}) %collective-permute-start.1) | collective-permute-done | bytes 1048608 | tf_op jit(solution)/shard_map/ppermute | solution.py:16
  96.1 0.0 collective-permute-start.2
  96.1 0.0 copy-done.8
  96.2 21.2 %collective-permute-done.2 = bf16[512,1024]{1,0:T(8,128)(2,1)} collective-permute-done((bf16[512,1024]{1,0:T(8,128)(2,1)S(1)}, bf16[512,1024]{1,0:T(8,128)(2,1)}, u32[]{:S(2)}, u32[]{:S(2)}) %collective-permute-start.2) | collective-permute-done | bytes 1048608 | tf_op jit(solution)/shard_map/ppermute | solution.py:16
  117.4 1.3 constant_dynamic-update-slice_fusion.7
  118.7 0.1 constant_dynamic-update-slice_fusion.6
  118.8 0.1 constant_dynamic-update-slice_fusion.5
  118.9 0.1 constant_dynamic-update-slice_fusion.4
  119.0 1.3 constant_dynamic-update-slice_fusion.3
  120.3 0.1 constant_dynamic-update-slice_fusion.2
  120.4 0.1 constant_dynamic-update-slice_fusion.1
  120.5 0.1 constant_dynamic-update-slice_fusion
  120.6 0.0 copy-start.3
  120.6 3.4 copy-done.3
  124.0 0.9 fusion
  124.9 0.0 all-gather.4.cloned.1.call-done
  124.9 14.9 %fusion.27 = f32[512,1792]{1,0:T(8,128)} fusion(bf16[4096,1792]{1,0:T(8,128)(2,1)} %all-gather.4.cloned.1.call-done, f32[4096]{0:T(1024)S(1)} %convert_element_type.51, f32[512]{0:T(512)S(1)} %add_rsqrt_fusion, bf16[512,8192]{1,0:T(8,128)(2,1)} %copy-done.3, s32[]{:T(128)S(6)} %select_n.14), kind=kOutput, calls=%fused_computation.55 | convolution fusion | flops 7524581376 | bytes 22562820 | tf_op jit(solution)/shard_map/dot_general | solution.py:42
  139.8 35.8 %all-gather.6.cloned.1.call-done = bf16[4096,1792]{1,0:T(8,128)(2,1)} async-done(((bf16[512,1792]{1,0:T(8,128)(2,1)}), bf16[4096,1792]{1,0:T(8,128)(2,1)}) %all-gather.6.cloned.1.call-update) | async-done | bytes 14680080 | tf_op jit(solution)/shard_map/all_gather | solution.py:67
  175.6 85.6 %all-gather.8.cloned.1.call-done = bf16[1792,4096]{1,0:T(8,128)(2,1)} async-done(((bf16[1792,512]{1,0:T(8,128)(2,1)}), bf16[1792,4096]{1,0:T(8,128)(2,1)}) %all-gather.8.cloned.1.call-update) | async-done | bytes 14680080 | tf_op jit(solution)/shard_map/all_gather | solution.py:71
  261.3 28.8 %convolution_convert_fusion = bf16[512,4096]{1,0:T(8,128)(2,1)} fusion(bf16[1792,4096]{1,0:T(8,128)(2,1)} %all-gather.8.cloned.1.call-done, f32[512,1792]{1,0:T(8,128)} %fusion.27, bf16[4096,1792]{1,0:T(8,128)(2,1)} %all-gather.6.cloned.1.call-done, f32[4096]{0:T(1024)S(1)} %convert_element_type.51, f32[512]{0:T(512)S(1)} %add_rsqrt_fusion, ...), kind=kOutput, calls=%fused_computation.10 | convolution fusion | flops 15048376320 | bytes 41437188 | tf_op jit(solution)/shard_map/dot_general | solution.py:69
  290.0 0.0 copy-start.11
  290.0 0.0 copy-start.6
  290.0 0.0 copy-start.7
  290.0 0.0 reduce-scatter.2.cloned.1.call-update
  290.1 0.6 copy-done.11
  290.7 0.1 slice.120
  290.8 0.1 copy-done.6
  290.8 0.7 fusion.31
  291.6 0.0 copy-done.7
  291.6 2.1 while.10
  293.8 73.2 %reduce-scatter.2.cloned.1.call-done = bf16[512,1024]{1,0:T(8,128)(2,1)} async-done(((bf16[512,4096]{1,0:T(8,128)(2,1)}), bf16[512,1024]{1,0:T(8,128)(2,1)}) %reduce-scatter.2.cloned.1.call-update) | async-done | bytes 1048592 | tf_op jit(solution)/shard_map/reduce_scatter | solution.py:74
  367.0 0.0 copy-start.1
  367.0 4.7 %fusion.7 = (f32[1,512,1024]{2,1,0:T(8,128)S(1)}, f32[1,512,1024]{2,1,0:T(8,128)S(1)}) fusion(bf16[512,1024]{1,0:T(8,128)(2,1)} %reduce-scatter.2.cloned.1.call-done, f32[4,512,1024]{2,1,0:T(8,128)} %param.10, f32[512]{0:T(512)S(1)} %bitcast.105, f32[512]{0:T(512)S(1)} %bitcast.106, f32[512]{0:T(512)S(1)} %bitcast.107, f32[512]{0:T(512)S(1)} %bitcast.100, ...), kind=kLoop, calls=%fused_computation.20 | loop fusion | flops 9961472 | bytes 13651968 | tf_op jit(solution)/shard_map/stack | solution.py:83
  371.8 1.4 copy-done.1
  373.2 0.2 copy-done.2
  373.4 1.7 fusion.17
  375.1 3.7 pad_maximum_fusion
  (70 shorter events, 1.8 us)
Async XLA Ops:
  6.5 118.4 %all-gather.4.cloned.1.call-start = ((), (), s32[]{:S(2)}) async-start(), calls=%async_computation.1 | async-start | bytes 16515072 | tf_op jit(solution)/shard_map/all_gather | solution.py:66
  7.3 168.4 %all-gather.6.cloned.1.call-start = ((), (), s32[]{:S(2)}) async-start(), calls=%async_computation.2 | async-start | bytes 16515072 | tf_op jit(solution)/shard_map/all_gather | solution.py:67
  8.0 253.3 %all-gather.8.cloned.1.call-start = ((), (), s32[]{:S(2)}) async-start(), calls=%async_computation.3 | async-start | bytes 16515072 | tf_op jit(solution)/shard_map/all_gather | solution.py:71
  8.1 4.9 %copy-start.4 = (f32[24,4,1024]{2,1,0:T(4,128)S(1)}, f32[24,4,1024]{2,1,0:T(4,128)}, u32[]{:S(2)}) copy-start(f32[24,4,1024]{2,1,0:T(4,128)} %param.11) | copy-start | bytes 1179652
  8.7 358.3 %reduce-scatter.2.cloned.1.call-start = ((), (), s32[]{:S(2)}) async-start(), calls=%async_computation.4 | async-start | bytes 5242880 | tf_op jit(solution)/shard_map/reduce_scatter | solution.py:74
  8.8 5.8 %copy-start = (f32[4,512,1024]{2,1,0:T(8,128)S(1)}, f32[4,512,1024]{2,1,0:T(8,128)}, u32[]{:S(2)}) copy-start(f32[4,512,1024]{2,1,0:T(8,128)} %param.10) | copy-start | bytes 25165828
  14.6 28.0 %copy-start.9 = (f32[3]{0:T(128)S(1)}, f32[3]{0:T(128)}, u32[]{:S(2)}) copy-start(f32[3]{0:T(128)} %param.13) | copy-start | bytes 40
  14.6 28.6 %copy-start.10 = (f32[24]{0:T(128)S(1)}, f32[24]{0:T(128)}, u32[]{:S(2)}) copy-start(f32[24]{0:T(128)} %param.12) | copy-start | bytes 292
  43.3 2.0 copy-start.5
  45.3 50.8 %copy-start.8 = (bf16[4096]{0:T(1024)(128)(2,1)S(1)}, bf16[4096]{0:T(1024)(128)(2,1)}, u32[]{:S(2)}) copy-start(bf16[4096]{0:T(1024)(128)(2,1)} %param.14) | copy-start | bytes 24580
  49.4 23.4 %collective-permute-start = (bf16[512,1024]{1,0:T(8,128)(2,1)S(1)}, bf16[512,1024]{1,0:T(8,128)(2,1)S(1)}, u32[]{:S(2)}, u32[]{:S(2)}) collective-permute-start(bf16[512,1024]{1,0:T(8,128)(2,1)S(1)} %multiply_reduce_fusion), channel_id=1, source_target_pairs={{0,1},{1,2},{2,3},{3,0},{4,5},{5,6},{6,7},{7,4},{8,9},{9,10},{10,1... | collective-permute-start | bytes 3145736 | tf_op jit(solution)/shard_map/ppermute | solution.py:16
  72.8 23.3 %collective-permute-start.1 = (bf16[512,1024]{1,0:T(8,128)(2,1)S(1)}, bf16[512,1024]{1,0:T(8,128)(2,1)S(1)}, u32[]{:S(2)}, u32[]{:S(2)}) collective-permute-start(bf16[512,1024]{1,0:T(8,128)(2,1)S(1)} %collective-permute-done), channel_id=1, source_target_pairs={{0,1},{1,2},{2,3},{3,0},{4,5},{5,6},{6,7},{7,4},{8,9},{9,10},{10,1... | collective-permute-start | bytes 3145736 | tf_op jit(solution)/shard_map/ppermute | solution.py:16
  96.1 21.3 %collective-permute-start.2 = (bf16[512,1024]{1,0:T(8,128)(2,1)S(1)}, bf16[512,1024]{1,0:T(8,128)(2,1)}, u32[]{:S(2)}, u32[]{:S(2)}) collective-permute-start(bf16[512,1024]{1,0:T(8,128)(2,1)S(1)} %collective-permute-done.1), channel_id=1, source_target_pairs={{0,1},{1,2},{2,3},{3,0},{4,5},{5,6},{6,7},{7,4},{8,9},{9,10},{10,1... | collective-permute-start | bytes 3145736 | tf_op jit(solution)/shard_map/ppermute | solution.py:16
  120.6 3.4 copy-start.3
  290.0 0.7 copy-start.11
  290.0 0.8 copy-start.6
  290.0 1.5 copy-start.7
  367.0 6.1 %copy-start.1 = (f32[4,512,1024]{2,1,0:T(8,128)S(1)}, f32[4,512,1024]{2,1,0:T(8,128)}, u32[]{:S(2)}) copy-start(f32[4,512,1024]{2,1,0:T(8,128)} %param.10) | copy-start | bytes 25165828
  367.0 6.4 %copy-start.2 = (bf16[512,1024]{1,0:T(8,128)(2,1)S(1)}, bf16[512,1024]{1,0:T(8,128)(2,1)}, u32[]{:S(2)}) copy-start(bf16[512,1024]{1,0:T(8,128)(2,1)} %reduce-scatter.2.cloned.1.call-done) | copy-start | bytes 3145732
Sparse Core Ops, SparseCore 0:
  9.2 83.5 all-gather.3
  94.7 80.8 all-gather.5
  177.5 83.7 all-gather.7
  290.2 76.7 reduce-scatter.1
